TPU v7x, 256 devices: a whole 4x4x8 slice. The times are simulated.
256 devices in a mesh: track: 4 (over y), ifg: 4 (over z_lo), pix: 16 (over z_hi, x, core).
Axes of the slice: x: 4, y: 4, z: 8 (z_hi: 2, z_lo: 4; z = z_hi * 4 + z_lo), core: 2. Of those that a mesh axis runs over, the one named last changes fastest.
Arguments:
- phases: bfloat16 [4, 600, 262144], P('track', 'ifg', 'pix')
- pairs: int32 [4, 600, 2], P('track', 'ifg'), may hold values from 0 to 249, as said below
- date_map: int32 [4, 250], replicated, may hold values from 0 to 319, as said below
- knots: int32 [32], replicated, may hold values from 0 to 319, as said below
- look: float32 [4, 3, 262144], P(None, None, 'pix'), may hold values from -1 to 1
Outputs:
- enu: float32 [3, 320, 262144], P(None, None, ('pix', 'ifg', 'track'))
- spline: float32 [3, 32, 262144], P(None, None, ('pix', 'ifg', 'track'))
Inputs may be any that keep to these rules, and one draw needn't show every extreme that they name: pairs[t, k, 0] < pairs[t, k, 1] <= pairs[t, k, 0] + 5. `date_map`: the dates of one track map to distinct epochs. `knots`: strictly increasing, the first 0 and the last 319.
All inputs are finite; a program needn't handle non-finite values.
Results may differ from a plain program's by a relative error of at most 0.0003.
Values may be sent and summed in bfloat16 or wider, within the bound.
A program may use at most 128 MiB of HBM per device.

v0:
```python
import jax
import jax.numpy as jnp
from jax import lax
from jax.sharding import PartitionSpec as P

EPOCHS = 320
damping = 0.5
ridge = 0.1
HIGH = lax.Precision.HIGHEST


def joined_along(tiles, dim):
    tiles = jnp.moveaxis(tiles, 0, dim)
    lengths = tiles.shape
    return tiles.reshape(*lengths[:dim], lengths[dim] * lengths[dim + 1], *lengths[dim + 2 :])


def from_everyone(value, axis):
    copies = jnp.broadcast_to(value, (lax.axis_size(axis), *value.shape))
    return lax.all_to_all(copies, axis, split_axis=0, concat_axis=0, tiled=True)


def collect(value, axis, dim):
    return joined_along(from_everyone(value, axis), dim)


def taken_together(value, axis):
    everything = from_everyone(value, axis)
    return jnp.sum(everything, axis=0)


def incidence(pair_rows, ndate):
    dates = jnp.arange(ndate, dtype=jnp.int32)[:, None]
    later = (dates == pair_rows[None, :, 1]).astype(jnp.float32)
    earlier = (dates == pair_rows[None, :, 0]).astype(jnp.float32)
    return later - earlier


def inverse_normal(normal_part):
    ndate = normal_part.shape[0]
    normal = normal_part + damping * jnp.eye(ndate, dtype=jnp.float32)
    factor = jnp.linalg.cholesky(normal)
    return jax.scipy.linalg.cho_solve((factor, True), jnp.eye(ndate, dtype=jnp.float32))


def hat_basis(knots, n_epochs):
    spots = knots.astype(jnp.float32)
    left = jnp.concatenate([spots[:1] - 1.0, spots[:-1]])
    right = jnp.concatenate([spots[1:], spots[-1:] + 1.0])
    epochs = jnp.arange(n_epochs, dtype=jnp.float32)[:, None]
    rise = (epochs - left) / (spots - left)
    fall = (right - epochs) / (right - spots)
    return jnp.maximum(0.0, jnp.minimum(rise, fall))


def geometry(series, date_map, look, knots, n_epochs):
    epochs = jnp.arange(n_epochs, dtype=jnp.int32)
    onehot = (date_map[:, None, :] == epochs[None, :, None]).astype(jnp.float32)
    seen = jnp.sum(onehot, axis=2)
    resampled = jnp.einsum("tcd,tdp->tcp", onehot, series, precision=HIGH)

    def entry(first, second):
        value = jnp.einsum("tc,tp->cp", seen, look[:, first] * look[:, second], precision=HIGH)
        if first == second:
            value = value + ridge
        return value

    a00, a01, a02 = (entry(0, 0), entry(0, 1), entry(0, 2))
    a11, a12, a22 = (entry(1, 1), entry(1, 2), entry(2, 2))
    b_all = [jnp.sum(look[:, i][:, None, :] * resampled, axis=0) for i in range(3)]
    c00 = a11 * a22 - a12 * a12
    c01 = a02 * a12 - a01 * a22
    c02 = a01 * a12 - a02 * a11
    c11 = a00 * a22 - a02 * a02
    c12 = a01 * a02 - a00 * a12
    c22 = a00 * a11 - a01 * a01
    det = a00 * c00 + a01 * c01 + a02 * c02
    east = (c00 * b_all[0] + c01 * b_all[1] + c02 * b_all[2]) / det
    north = (c01 * b_all[0] + c11 * b_all[1] + c12 * b_all[2]) / det
    upward = (c02 * b_all[0] + c12 * b_all[1] + c22 * b_all[2]) / det
    enu = jnp.stack([east, north, upward])
    basis = hat_basis(knots, n_epochs)
    gram = jnp.dot(basis.T, basis, precision=HIGH)
    factor = jnp.linalg.cholesky(gram)
    fitter = jax.scipy.linalg.cho_solve((factor, True), basis.T)
    spline = jnp.einsum("kc,icp->ikp", fitter, enu, precision=HIGH)
    return (enu, spline)


def shards(phases, pairs, date_map, knots, look):
    ndate = date_map.shape[1]
    n_epochs = hat_count()
    n_track = lax.axis_size("track")
    n_ifg = lax.axis_size("ifg")
    width = phases.shape[2] // (n_track * n_ifg)
    offset = lax.axis_index("ifg") * (width * n_track) + lax.axis_index("track") * width
    look_local = lax.dynamic_slice_in_dim(look, offset, width, 2)
    phase_rows = phases[0]
    pair_rows = pairs[0]
    phase_all = lax.all_to_all(phase_rows, "ifg", split_axis=1, concat_axis=0, tiled=True)
    pair_all = collect(pair_rows, "ifg", 0)
    incid = incidence(pair_all, ndate)
    normal_part = jnp.dot(incid, incid.T, precision=HIGH)
    rhs = jnp.dot(incid.astype(jnp.bfloat16), phase_all, preferred_element_type=jnp.float32)
    ninv = inverse_normal(normal_part)
    pixel_count = rhs.shape[1] * lax.axis_size("ifg") * lax.axis_size("pix")
    series = jnp.dot(ninv, rhs, precision=HIGH)
    total = taken_together(jnp.sum(series, axis=1), ("ifg", "pix"))
    series = series - (total / pixel_count)[:, None]
    gathered = lax.all_to_all(series[None], "track", split_axis=2, concat_axis=0, tiled=True)
    return geometry(gathered, date_map, look_local, knots, n_epochs)


def hat_count():
    return EPOCHS


def solution(mesh):
    in_specs = (P("track", "ifg", "pix"), P("track", "ifg", None), P(), P(), P(None, None, "pix"))
    out_specs = (P(None, None, ("pix", "ifg", "track")), P(None, None, ("pix", "ifg", "track")))
    return jax.shard_map(shards, mesh=mesh, in_specs=in_specs, out_specs=out_specs, check_vma=False)
```

profile of v0, /device:TPU:1, one launch (start us, length us, event | category | flops | bytes accessed | tf_op | source)
XLA Modules:
  0.0 270.9 jit_solution(16111083648875466656)
XLA Ops:
  0.6 1.3 broadcast_in_dim.9
  1.9 6.4 %all-to-all-start = ((s32[4,150,2]{1,2,0:T(2,128)}), s32[4,150,2]{1,2,0:T(2,128)S(1)}, u32[]{:S(2)}, u32[]{:S(2)}) async-start(s32[4,150,2]{1,2,0:T(2,128)} %broadcast_in_dim.9), calls=%async_computation | async-start | bytes 16384 | tf_op jit(solution)/shard_map/all_to_all | solution.py:20
  8.3 11.1 %all_to_all.35 = bf16[150,4,4096]{2,1,0:T(4,128)(2,1)} reshape(bf16[1,150,16384]{2,1,0:T(8,128)(2,1)} %param.5) | data formatting | bytes 9830400 | tf_op jit(solution)/shard_map/all_to_all | solution.py:100
  19.4 7.3 %copy.30 = bf16[150,4,4096]{2,0,1:T(8,128)(2,1)} copy(bf16[150,4,4096]{2,1,0:T(4,128)(2,1)} %all_to_all.35) | data formatting | bytes 9830400 | tf_op jit(solution)/shard_map/all_to_all | solution.py:100
  26.8 5.4 %all-to-all-start.1 = ((bf16[150,4,4096]{2,0,1:T(8,128)(2,1)}), bf16[150,4,4096]{2,0,1:T(8,128)(2,1)}, u32[]{:S(2)}, u32[]{:S(2)}) async-start(bf16[150,4,4096]{2,0,1:T(8,128)(2,1)} %copy.30), calls=%async_computation.1 | async-start | bytes 9961472 | tf_op jit(solution)/shard_map/all_to_all | solution.py:100
  32.4 1.0 fusion.3
  33.7 11.7 %cholesky.63 = f32[128,128]{1,0:T(8,128)S(1)} custom-call(f32[128,128]{1,0:T(8,128)S(1)} %cholesky.156), custom_call_target="Cholesky" | custom-call | tf_op jit(solution)/shard_map/jit(cholesky)/cholesky | solution.py:42
  45.4 9.8 %custom-call.28 = f32[1,128,128]{1,2,0:T(8,128)S(1)} custom-call(f32[1,128,128]{2,1,0:T(8,128)S(1)} %get-tuple-element.40), custom_call_target="InvertDiagBlocksLowerTriangular" | custom-call | tf_op jit(solution)/shard_map/jit(cholesky)/cholesky | solution.py:42
  55.5 0.3 convolution_subtract_fusion.2
  55.7 11.2 %cholesky.133 = f32[122,122]{1,0:T(8,128)S(1)} custom-call(f32[122,122]{1,0:T(8,128)S(1)} %convolution_subtract_fusion.2), custom_call_target="Cholesky" | custom-call | tf_op jit(solution)/shard_map/jit(cholesky)/cholesky | solution.py:42
  66.9 0.6 compare_reduce_fusion.1
  67.6 0.6 compare_reduce_fusion.2
  69.7 20.2 %custom-call.29 = f32[2,128,128]{1,2,0:T(8,128)S(1)} custom-call(f32[2,128,128]{2,1,0:T(8,128)S(1)} %pad_maximum_fusion.1), custom_call_target="InvertDiagBlocksLowerTriangular" | custom-call | tf_op jit(solution)/shard_map/jit(_cho_solve)/triangular_solve | solution.py:43
  89.9 0.3 fusion.17
  90.2 0.3 convolution_subtract_fusion.1
  90.4 0.3 fusion.27
  91.0 0.3 convolution_subtract_fusion
  91.6 50.3 %all-to-all-done.1 = bf16[150,4,4096]{2,0,1:T(8,128)(2,1)} async-done(((bf16[150,4,4096]{2,0,1:T(8,128)(2,1)}), bf16[150,4,4096]{2,0,1:T(8,128)(2,1)}, u32[]{:S(2)}, u32[]{:S(2)}) %all-to-all-start.1) | async-done | bytes 4915232 | tf_op jit(solution)/shard_map/all_to_all | solution.py:100
  141.9 6.0 %all_to_all.38 = bf16[600,4096]{1,0:T(8,128)(2,1)} reshape(bf16[4,150,4096]{2,1,0:T(8,128)(2,1)} %bitcast.11) | data formatting | bytes 9830400 | tf_op jit(solution)/shard_map/all_to_all | solution.py:100
  147.8 4.2 %fusion.5 = f32[250,4096]{1,0:T(8,128)S(1)} fusion(bf16[600,4096]{1,0:T(8,128)(2,1)} %all_to_all.38, s32[600]{0:T(1024)S(1)} %get-tuple-element.26, s32[600]{0:T(1024)S(1)} %get-tuple-element.25), kind=kOutput, calls=%fused_computation.31 | convolution fusion | flops 1229699968 | bytes 9016000 | tf_op jit(solution)/shard_map/dot_general | solution.py:104
  152.0 5.3 %fusion.48 = (f32[250]{0:T(256)S(1)}, f32[250,4096]{1,0:T(8,128)}) fusion(f32[250,4096]{1,0:T(8,128)S(1)} %fusion.5, f32[122,250]{1,0:T(8,128)S(1)} %fusion.26, f32[128,250]{1,0:T(8,128)S(1)} %fusion.25), kind=kOutput, calls=%fused_computation.113 | convolution fusion | flops 3073086208 | bytes 8443000 | tf_op jit(solution)/shard_map/dot_general | solution.py:107
  157.3 0.7 broadcast_in_dim.10
  158.0 10.5 %all-to-all-start.2 = ((f32[64,1,250]{2,1,0:T(1,128)}), f32[64,1,250]{2,1,0:T(1,128)S(1)}, u32[]{:S(2)}, u32[]{:S(2)}) async-start(f32[64,1,250]{2,1,0:T(1,128)} %broadcast_in_dim.10), calls=%async_computation.2 | async-start | bytes 131072 | tf_op jit(solution)/shard_map/all_to_all | solution.py:20
  168.6 9.6 %all-to-all-done.2 = f32[64,1,250]{2,1,0:T(1,128)S(1)} async-done(((f32[64,1,250]{2,1,0:T(1,128)}), f32[64,1,250]{2,1,0:T(1,128)S(1)}, u32[]{:S(2)}, u32[]{:S(2)}) %all-to-all-start.2) | async-done | bytes 64032 | tf_op jit(solution)/shard_map/all_to_all | solution.py:20
  178.3 4.7 %subtract_bitcast_fusion = f32[1,250,4096]{2,1,0:T(8,128)} fusion(f32[250,4096]{1,0:T(8,128)} %get-tuple-element.50, f32[250]{0:T(256)S(1)} %broadcast_multiply_fusion), kind=kLoop, calls=%fused_computation.5 | loop fusion | flops 1024000 | bytes 8193000 | tf_op jit(solution)/shard_map/broadcast_in_dim | solution.py:110
  183.0 10.2 %copy.32 = f32[1,250,4096]{1,0,2:T(1,128)} copy(f32[1,250,4096]{2,1,0:T(8,128)} %subtract_bitcast_fusion) | data formatting | bytes 8192000 | tf_op jit(solution)/shard_map/broadcast_in_dim | solution.py:110
  193.2 5.0 %all-to-all-start.3 = ((f32[1,250,4096]{1,0,2:T(1,128)}), f32[1,250,4096]{1,0,2:T(1,128)}, u32[]{:S(2)}, u32[]{:S(2)}) async-start(f32[1,250,4096]{1,0,2:T(1,128)} %copy.32), calls=%async_computation.3 | async-start | bytes 8388608 | tf_op jit(solution)/shard_map/all_to_all | solution.py:110
  198.2 0.6 fusion.46
  200.2 0.4 fusion.20
  200.7 2.9 %cholesky.147 = f32[32,32]{1,0:T(8,128)S(1)} custom-call(f32[32,32]{1,0:T(8,128)S(1)} %fusion.33), custom_call_target="Cholesky" | custom-call | tf_op jit(solution)/shard_map/jit(cholesky)/cholesky | solution.py:84
  203.7 0.6 compare_reduce_fusion
  204.3 0.7 fusion.30
  205.0 2.4 custom-call.30
  207.4 0.8 dynamic-slice_bitcast_fusion.2
  208.2 0.3 fusion.19
  208.8 0.3 convert_reduce_fusion
  209.1 2.4 convolution_add_fusion
  211.4 2.4 convolution_add_fusion.1
  213.8 2.3 convolution_add_fusion.2
  216.1 1.2 fusion.35
  217.4 1.3 fusion.37
  218.7 28.1 %all-to-all-done.3 = f32[1,250,4096]{1,0,2:T(1,128)} async-done(((f32[1,250,4096]{1,0,2:T(1,128)}), f32[1,250,4096]{1,0,2:T(1,128)}, u32[]{:S(2)}, u32[]{:S(2)}) %all-to-all-start.3) | async-done | bytes 4096032 | tf_op jit(solution)/shard_map/all_to_all | solution.py:110
  246.8 4.4 %copy.35 = f32[1,250,4096]{1,2,0:T(8,128)} copy(f32[1,250,4096]{1,0,2:T(1,128)} %all-to-all-done.3) | data formatting | bytes 8192000
  251.2 5.6 %copy.33 = f32[1,250,4,1024]{3,1,2,0:T(8,128)} copy(f32[1,250,4,1024]{1,3,2,0:T(8,128)} %bitcast.84) | data formatting | bytes 8192000 | tf_op jit(solution)/shard_map/all_to_all | solution.py:110
  256.9 6.9 %multiply_reduce_fusion.2 = (f32[320,1024]{1,0:T(8,128)S(1)}, f32[320,1024]{1,0:T(8,128)S(1)}, f32[320,1024]{1,0:T(8,128)S(1)}) fusion(f32[4,1024]{1,0:T(4,128)S(1)} %get-tuple-element.36, f32[4,1024]{1,0:T(4,128)S(1)} %get-tuple-element.35, f32[4,1024]{1,0:T(4,128)S(1)} %get-tuple-element.34, f32[1,250,4,1024]{3,1,2,0:T(8,128)} %copy.33, ...), kind=kOutput, calls=%fused_computation.2 | convolution fusion | flops 3939361280 | bytes 8081312 | tf_op jit(solution)/shard_map/tcd,tdp->tcp/dot_general | solution.py:60
  263.8 3.0 %divide_bitcast_fusion.2 = (f32[1,320,1024]{2,1,0:T(8,128)S(1)}, f32[1,320,1024]{2,1,0:T(8,128)S(1)}, f32[1,320,1024]{2,1,0:T(8,128)S(1)}) fusion(f32[320,1024]{1,0:T(8,128)S(1)} %get-tuple-element.23, f32[320,1024]{1,0:T(8,128)S(1)} %get-tuple-element.24, f32[320,1024]{1,0:T(8,128)S(1)} %get-tuple-element.22, f32[320,1024]{1,0:T(8,128)S(1)} %copy-done.3, ...), kind=kOutput, calls=%fused_computation.13 | convolution fusion | flops 29167616 | bytes 14455808 | tf_op jit(solution)/shard_map/tc,tp->cp/dot_general | solution.py:63
  266.8 0.5 pad_maximum_fusion
  267.3 3.3 %convolution_bitcast_fusion = f32[3,32,1024]{2,1,0:T(8,128)} fusion(f32[3,320,1024]{2,1,0:T(8,128)S(1)} %pad_maximum_fusion, f32[32,320,1]{1,0,2:T(8,128)S(1)} %convolution_bitcast_fusion.1), kind=kOutput, calls=%fused_computation.20 | convolution fusion | flops 377487360 | bytes 4366336 | tf_op jit(solution)/shard_map/kc,icp->ikp/dot_general | solution.py:86
  (41 shorter events, 1.9 us)
Async XLA Ops:
  1.9 24.9 %all-to-all-start = ((s32[4,150,2]{1,2,0:T(2,128)}), s32[4,150,2]{1,2,0:T(2,128)S(1)}, u32[]{:S(2)}, u32[]{:S(2)}) async-start(s32[4,150,2]{1,2,0:T(2,128)} %broadcast_in_dim.9), calls=%async_computation | async-start | bytes 16384 | tf_op jit(solution)/shard_map/all_to_all | solution.py:20
  26.8 5.4 %copy-start.5 = (s32[32]{0:T(128)S(1)}, s32[32]{0:T(128)}, u32[]{:S(2)}) copy-start(s32[32]{0:T(128)} %param.8) | copy-start | bytes 388
  26.8 115.1 %all-to-all-start.1 = ((bf16[150,4,4096]{2,0,1:T(8,128)(2,1)}), bf16[150,4,4096]{2,0,1:T(8,128)(2,1)}, u32[]{:S(2)}, u32[]{:S(2)}) async-start(bf16[150,4,4096]{2,0,1:T(8,128)(2,1)} %copy.30), calls=%async_computation.1 | async-start | bytes 9961472 | tf_op jit(solution)/shard_map/all_to_all | solution.py:100
  158.0 20.2 %all-to-all-start.2 = ((f32[64,1,250]{2,1,0:T(1,128)}), f32[64,1,250]{2,1,0:T(1,128)S(1)}, u32[]{:S(2)}, u32[]{:S(2)}) async-start(f32[64,1,250]{2,1,0:T(1,128)} %broadcast_in_dim.10), calls=%async_computation.2 | async-start | bytes 131072 | tf_op jit(solution)/shard_map/all_to_all | solution.py:20
  193.2 53.6 %all-to-all-start.3 = ((f32[1,250,4096]{1,0,2:T(1,128)}), f32[1,250,4096]{1,0,2:T(1,128)}, u32[]{:S(2)}, u32[]{:S(2)}) async-start(f32[1,250,4096]{1,0,2:T(1,128)} %copy.32), calls=%async_computation.3 | async-start | bytes 8388608 | tf_op jit(solution)/shard_map/all_to_all | solution.py:110
  200.2 8.6 %copy-start.4 = (s32[4,250]{1,0:T(4,128)S(1)}, s32[4,250]{1,0:T(4,128)}, u32[]{:S(2)}) copy-start(s32[4,250]{1,0:T(4,128)} %param.7) | copy-start | bytes 12004
  256.8 6.9 %copy-start.1 = (f32[320,1024]{1,0:T(8,128)S(1)}, f32[320,1024]{1,0:T(8,128)}, u32[]{:S(2)}) copy-start(f32[320,1024]{1,0:T(8,128)} %convolution_add_fusion) | copy-start | bytes 3932164
  256.8 6.9 %copy-start.2 = (f32[320,1024]{1,0:T(8,128)S(1)}, f32[320,1024]{1,0:T(8,128)}, u32[]{:S(2)}) copy-start(f32[320,1024]{1,0:T(8,128)} %convolution_add_fusion.1) | copy-start | bytes 3932164
  256.8 6.9 %copy-start.3 = (f32[320,1024]{1,0:T(8,128)S(1)}, f32[320,1024]{1,0:T(8,128)}, u32[]{:S(2)}) copy-start(f32[320,1024]{1,0:T(8,128)} %convolution_add_fusion.2) | copy-start | bytes 3932164
  267.3 3.3 %copy-start = (f32[3,320,1024]{2,1,0:T(8,128)}, f32[3,320,1024]{2,1,0:T(8,128)S(1)}, u32[]{:S(2)}) copy-start(f32[3,320,1024]{2,1,0:T(8,128)S(1)} %pad_maximum_fusion) | copy-start | bytes 11796484
where the time goes:
time: 276 us; the launch traced here: 271 us
  waiting for transfers between devices  88 us (32%)
  other arithmetic  66.9 us (24%)
  local copies, waits for them, and re-layouts  48.4 us (18%)
  matrix products  36.4 us (13%)
  starting transfers between devices  27.3 us (10%)
  between operations  3.84 us (1%)
    all_to_all x1, waiting for transfers between devices, shards(): lax.all_to_all(phase_rows, 'ifg', split_axis=1, concat_axis=0, tiled=True)  50.3 us
    another operation x7, other arithmetic, inverse_normal(): factor = jnp.linalg.cholesky(normal)  34 us
    all_to_all x1, waiting for transfers between devices, shards(): lax.all_to_all(series[None], 'track', split_axis=2, concat_axis=0, tiled=...  28.1 us
    all_to_all x3, local copies, waits for them, and re-layouts, shards(): lax.all_to_all(phase_rows, 'ifg', split_axis=1, concat_axis=0, tiled=True)  24.4 us
    another operation x6, other arithmetic, inverse_normal(): jax.scipy.linalg.cho_solve((factor, True), jnp.eye(ndate, dtype=jnp.float...  20.3 us
    all_to_all x2, starting transfers between devices, from_everyone(): return lax.all_to_all(copies, axis, split_axis=0, concat_axis=0, tiled=True)  16.9 us
    dot_general x6, matrix products, entry(): jnp.einsum('tc,tp->cp', seen, look[:, first] * look[:, second], precision...  12.6 us
    broadcast_in_dim x1, local copies, waits for them, and re-layouts, shards(): series[None]  10.2 us
  transfers between devices with their start and end apart: 4, of which 3 were waited for; matrix products, arithmetic and copies ran while one was open for 31% of the time, Pallas kernels for 0%

commit v1 on v0

--- a/solution.py
+++ b/solution.py
@@ -107,7 +107,12 @@
     series = jnp.dot(ninv, rhs, precision=HIGH)
     total = taken_together(jnp.sum(series, axis=1), ("ifg", "pix"))
     series = series - (total / pixel_count)[:, None]
-    gathered = lax.all_to_all(series[None], "track", split_axis=2, concat_axis=0, tiled=True)
+    gathered = jnp.concatenate(
+        lax.all_to_all(
+            jnp.stack(jnp.split(series[None], lax.axis_size("track"), axis=2)), "track", 0, 0
+        ),
+        axis=0,
+    )
     return geometry(gathered, date_map, look_local, knots, n_epochs)
 
 

time: 276 us -> 260 us (0.942)
  local copies, waits for them, and re-layouts: 48.4 us -> 34.8 us
    broadcast_in_dim x1 -> x0, local copies, waits for them, and re-layouts: 10.2 us -> none  [shards(): series[None]]
    another operation x0 -> x2, local copies, waits for them, and re-layouts: none -> 6.7 us  [shards(): jnp.stack(jnp.split(series[None], lax.axis_size('track'), axis=2))]
    all_to_all x1 -> x0, local copies, waits for them, and re-layouts: 5.6 us -> none  [shards(): lax.all_to_all(series[None], 'track', split_axis=2, concat_axis=0, tiled=...]
    unnamed x13 -> x12, local copies, waits for them, and re-layouts: 4.46 us -> 0.02 us
  transfers between devices with their start and end apart: 4 -> 4, of which waited for: 3 -> 3; matrix products, arithmetic and copies ran while one was open for 31% -> 33% of each run, Pallas kernels for 0% -> 0%
where the time goes in v1:
time: 260 us; the launch traced here: 255 us
  waiting for transfers between devices  87.2 us (34%)
  other arithmetic  64.8 us (25%)
  matrix products  36.8 us (14%)
  local copies, waits for them, and re-layouts  34.8 us (13%)
  starting transfers between devices  27.6 us (11%)
  between operations  4.04 us (2%)
    all_to_all x1, waiting for transfers between devices, shards(): lax.all_to_all(phase_rows, 'ifg', split_axis=1, concat_axis=0, tiled=True)  50.6 us
    another operation x7, other arithmetic, inverse_normal(): factor = jnp.linalg.cholesky(normal)  34 us
    all_to_all x1, waiting for transfers between devices, shards(): lax.all_to_all(jnp.stack(jnp.split(series[None], lax.axis_size('track'),...  26.9 us
    all_to_all x3, local copies, waits for them, and re-layouts, shards(): lax.all_to_all(phase_rows, 'ifg', split_axis=1, concat_axis=0, tiled=True)  24.4 us
    another operation x6, other arithmetic, inverse_normal(): jax.scipy.linalg.cho_solve((factor, True), jnp.eye(ndate, dtype=jnp.float...  20 us
    all_to_all x2, starting transfers between devices, from_everyone(): return lax.all_to_all(copies, axis, split_axis=0, concat_axis=0, tiled=True)  16.9 us
    dot_general x6, matrix products, entry(): jnp.einsum('tc,tp->cp', seen, look[:, first] * look[:, second], precision...  12.8 us
    all_to_all x2, waiting for transfers between devices, from_everyone(): return lax.all_to_all(copies, axis, split_axis=0, concat_axis=0, tiled=True)  9.64 us
  transfers between devices with their start and end apart: 4, of which 3 were waited for; matrix products, arithmetic and copies ran while one was open for 33% of the time, Pallas kernels for 0%

profile of v1, /device:TPU:1, one launch (start us, length us, event | category | flops | bytes accessed | tf_op | source)
XLA Modules:
  0.0 255.3 jit_solution(13472195605626599987)
XLA Ops:
  0.6 1.3 broadcast_in_dim.9
  1.9 6.4 %all-to-all-start = ((s32[4,150,2]{1,2,0:T(2,128)}), s32[4,150,2]{1,2,0:T(2,128)S(1)}, u32[]{:S(2)}, u32[]{:S(2)}) async-start(s32[4,150,2]{1,2,0:T(2,128)} %broadcast_in_dim.9), calls=%async_computation | async-start | bytes 16384 | tf_op jit(solution)/shard_map/all_to_all | solution.py:20
  8.3 11.1 %all_to_all.25 = bf16[150,4,4096]{2,1,0:T(4,128)(2,1)} reshape(bf16[1,150,16384]{2,1,0:T(8,128)(2,1)} %param.5) | data formatting | bytes 9830400 | tf_op jit(solution)/shard_map/all_to_all | solution.py:100
  19.4 7.3 %copy.30 = bf16[150,4,4096]{2,0,1:T(8,128)(2,1)} copy(bf16[150,4,4096]{2,1,0:T(4,128)(2,1)} %all_to_all.25) | data formatting | bytes 9830400 | tf_op jit(solution)/shard_map/all_to_all | solution.py:100
  26.8 5.6 %all-to-all-start.1 = ((bf16[150,4,4096]{2,0,1:T(8,128)(2,1)}), bf16[150,4,4096]{2,0,1:T(8,128)(2,1)}, u32[]{:S(2)}, u32[]{:S(2)}) async-start(bf16[150,4,4096]{2,0,1:T(8,128)(2,1)} %copy.30), calls=%async_computation.1 | async-start | bytes 9961472 | tf_op jit(solution)/shard_map/all_to_all | solution.py:100
  32.7 1.0 fusion.4
  33.9 11.7 %cholesky.63 = f32[128,128]{1,0:T(8,128)S(1)} custom-call(f32[128,128]{1,0:T(8,128)S(1)} %cholesky.156), custom_call_target="Cholesky" | custom-call | tf_op jit(solution)/shard_map/jit(cholesky)/cholesky | solution.py:42
  45.6 9.8 %custom-call.28 = f32[1,128,128]{1,2,0:T(8,128)S(1)} custom-call(f32[1,128,128]{2,1,0:T(8,128)S(1)} %get-tuple-element.44), custom_call_target="InvertDiagBlocksLowerTriangular" | custom-call | tf_op jit(solution)/shard_map/jit(cholesky)/cholesky | solution.py:42
  55.7 0.3 convolution_subtract_fusion.2
  56.0 11.2 %cholesky.133 = f32[122,122]{1,0:T(8,128)S(1)} custom-call(f32[122,122]{1,0:T(8,128)S(1)} %convolution_subtract_fusion.2), custom_call_target="Cholesky" | custom-call | tf_op jit(solution)/shard_map/jit(cholesky)/cholesky | solution.py:42
  67.2 0.6 compare_reduce_fusion.1
  67.8 0.6 compare_reduce_fusion.2
  69.9 19.8 %custom-call.29 = f32[2,128,128]{1,2,0:T(8,128)S(1)} custom-call(f32[2,128,128]{2,1,0:T(8,128)S(1)} %pad_maximum_fusion.2), custom_call_target="InvertDiagBlocksLowerTriangular" | custom-call | tf_op jit(solution)/shard_map/jit(_cho_solve)/triangular_solve | solution.py:43
  89.8 0.3 fusion.18
  90.3 0.3 fusion.28
  90.6 0.3 fusion.27
  90.9 0.3 convolution_subtract_fusion
  91.5 50.6 %all-to-all-done.1 = bf16[150,4,4096]{2,0,1:T(8,128)(2,1)} async-done(((bf16[150,4,4096]{2,0,1:T(8,128)(2,1)}), bf16[150,4,4096]{2,0,1:T(8,128)(2,1)}, u32[]{:S(2)}, u32[]{:S(2)}) %all-to-all-start.1) | async-done | bytes 4915232 | tf_op jit(solution)/shard_map/all_to_all | solution.py:100
  142.1 6.0 %all_to_all.28 = bf16[600,4096]{1,0:T(8,128)(2,1)} reshape(bf16[4,150,4096]{2,1,0:T(8,128)(2,1)} %bitcast.11) | data formatting | bytes 9830400 | tf_op jit(solution)/shard_map/all_to_all | solution.py:100
  148.0 4.2 %fusion.6 = f32[250,4096]{1,0:T(8,128)S(1)} fusion(bf16[600,4096]{1,0:T(8,128)(2,1)} %all_to_all.28, s32[600]{0:T(1024)S(1)} %get-tuple-element.26, s32[600]{0:T(1024)S(1)} %get-tuple-element.25), kind=kOutput, calls=%fused_computation.37 | convolution fusion | flops 1229699968 | bytes 9016000 | tf_op jit(solution)/shard_map/dot_general | solution.py:104
  152.3 5.3 %fusion.49 = (f32[250]{0:T(256)S(1)}, f32[250,4096]{1,0:T(8,128)}) fusion(f32[250,4096]{1,0:T(8,128)S(1)} %fusion.6, f32[122,250]{1,0:T(8,128)S(1)} %fusion.27, f32[128,250]{1,0:T(8,128)S(1)} %fusion.26), kind=kOutput, calls=%fused_computation.119 | convolution fusion | flops 3073086208 | bytes 8443000 | tf_op jit(solution)/shard_map/dot_general | solution.py:107
  157.5 0.7 broadcast_in_dim.10
  158.2 10.5 %all-to-all-start.2 = ((f32[64,1,250]{2,1,0:T(1,128)}), f32[64,1,250]{2,1,0:T(1,128)S(1)}, u32[]{:S(2)}, u32[]{:S(2)}) async-start(f32[64,1,250]{2,1,0:T(1,128)} %broadcast_in_dim.10), calls=%async_computation.2 | async-start | bytes 131072 | tf_op jit(solution)/shard_map/all_to_all | solution.py:20
  168.7 9.6 %all-to-all-done.2 = f32[64,1,250]{2,1,0:T(1,128)S(1)} async-done(((f32[64,1,250]{2,1,0:T(1,128)}), f32[64,1,250]{2,1,0:T(1,128)S(1)}, u32[]{:S(2)}, u32[]{:S(2)}) %all-to-all-start.2) | async-done | bytes 64032 | tf_op jit(solution)/shard_map/all_to_all | solution.py:20
  178.5 2.6 %subtract_bitcast_fusion = f32[1,250,4096]{2,1,0:T(8,128)S(1)} fusion(f32[250,4096]{1,0:T(8,128)} %get-tuple-element.54, f32[250]{0:T(256)S(1)} %broadcast_multiply_fusion), kind=kLoop, calls=%fused_computation.7 | loop fusion | flops 1024000 | bytes 8193000 | tf_op jit(solution)/shard_map/broadcast_in_dim | solution.py:112
  181.1 0.6 slice_bitcast_fusion.3
  181.7 0.3 pad_maximum_fusion
  182.0 6.1 %copy.32 = f32[4,1,250,1024]{3,1,2,0:T(1,128)} copy(f32[4,1,250,1024]{3,2,1,0:T(8,128)S(1)} %pad_maximum_fusion) | data formatting | bytes 8192000 | tf_op jit(solution)/shard_map/stack | solution.py:112
  188.2 5.0 %all-to-all-start.3 = ((f32[4,1,250,1024]{3,1,2,0:T(1,128)}), f32[4,1,250,1024]{3,1,2,0:T(1,128)}, u32[]{:S(2)}, u32[]{:S(2)}) async-start(f32[4,1,250,1024]{3,1,2,0:T(1,128)} %copy.32), calls=%async_computation.3 | async-start | bytes 8192000 | tf_op jit(solution)/shard_map/all_to_all | solution.py:111
  193.2 0.6 fusion.47
  195.2 0.4 fusion.21
  195.7 2.9 %cholesky.147 = f32[32,32]{1,0:T(8,128)S(1)} custom-call(f32[32,32]{1,0:T(8,128)S(1)} %fusion.34), custom_call_target="Cholesky" | custom-call | tf_op jit(solution)/shard_map/jit(cholesky)/cholesky | solution.py:84
  198.7 0.6 compare_reduce_fusion
  199.3 0.7 fusion.31
  200.0 2.4 custom-call.30
  202.4 0.8 dynamic-slice_bitcast_fusion.2
  203.2 0.3 fusion.20
  203.7 0.3 convert_reduce_fusion
  204.0 2.3 convolution_add_fusion
  206.3 2.4 convolution_add_fusion.1
  208.8 2.3 convolution_add_fusion.2
  211.1 1.2 fusion.36
  212.3 1.3 fusion.38
  213.6 26.9 %all-to-all-done.3 = f32[4,1,250,1024]{3,1,2,0:T(1,128)} async-done(((f32[4,1,250,1024]{3,1,2,0:T(1,128)}), f32[4,1,250,1024]{3,1,2,0:T(1,128)}, u32[]{:S(2)}, u32[]{:S(2)}) %all-to-all-start.3) | async-done | bytes 4096032 | tf_op jit(solution)/shard_map/all_to_all | solution.py:111
  240.5 7.1 %multiply_reduce_fusion.2 = (f32[320,1024]{1,0:T(8,128)S(1)}, f32[320,1024]{1,0:T(8,128)S(1)}, f32[320,1024]{1,0:T(8,128)S(1)}) fusion(f32[4,1024]{1,0:T(4,128)S(1)} %get-tuple-element.40, f32[4,1024]{1,0:T(4,128)S(1)} %get-tuple-element.39, f32[4,1024]{1,0:T(4,128)S(1)} %get-tuple-element.38, f32[4,1,250,1024]{3,1,2,0:T(1,128)} %all-to-all-done.3, ...), kind=kOutput, calls=%fused_computation.2 | convolution fusion | flops 3939361280 | bytes 8081312 | tf_op jit(solution)/shard_map/tcd,tdp->tcp/dot_general | solution.py:60
  247.7 3.3 %divide_bitcast_fusion.2 = (f32[1,320,1024]{2,1,0:T(8,128)S(1)}, f32[1,320,1024]{2,1,0:T(8,128)S(1)}, f32[1,320,1024]{2,1,0:T(8,128)S(1)}) fusion(f32[320,1024]{1,0:T(8,128)S(1)} %get-tuple-element.23, f32[320,1024]{1,0:T(8,128)S(1)} %get-tuple-element.24, f32[320,1024]{1,0:T(8,128)S(1)} %get-tuple-element.22, f32[320,1024]{1,0:T(8,128)S(1)} %copy-done.3, ...), kind=kOutput, calls=%fused_computation.15 | convolution fusion | flops 29167616 | bytes 14455808 | tf_op jit(solution)/shard_map/tc,tp->cp/dot_general | solution.py:63
  250.9 0.5 pad_maximum_fusion.1
  251.5 3.3 %convolution_bitcast_fusion = f32[3,32,1024]{2,1,0:T(8,128)} fusion(f32[3,320,1024]{2,1,0:T(8,128)S(1)} %pad_maximum_fusion.1, f32[32,320,1]{1,0,2:T(8,128)S(1)} %convolution_bitcast_fusion.1), kind=kOutput, calls=%fused_computation.22 | convolution fusion | flops 377487360 | bytes 4366336 | tf_op jit(solution)/shard_map/kc,icp->ikp/dot_general | solution.py:86
  (41 shorter events, 1.9 us)
Async XLA Ops:
  1.9 24.9 %all-to-all-start = ((s32[4,150,2]{1,2,0:T(2,128)}), s32[4,150,2]{1,2,0:T(2,128)S(1)}, u32[]{:S(2)}, u32[]{:S(2)}) async-start(s32[4,150,2]{1,2,0:T(2,128)} %broadcast_in_dim.9), calls=%async_computation | async-start | bytes 16384 | tf_op jit(solution)/shard_map/all_to_all | solution.py:20
  26.8 5.7 %copy-start.5 = (s32[32]{0:T(128)S(1)}, s32[32]{0:T(128)}, u32[]{:S(2)}) copy-start(s32[32]{0:T(128)} %param.8) | copy-start | bytes 388
  26.8 115.3 %all-to-all-start.1 = ((bf16[150,4,4096]{2,0,1:T(8,128)(2,1)}), bf16[150,4,4096]{2,0,1:T(8,128)(2,1)}, u32[]{:S(2)}, u32[]{:S(2)}) async-start(bf16[150,4,4096]{2,0,1:T(8,128)(2,1)} %copy.30), calls=%async_computation.1 | async-start | bytes 9961472 | tf_op jit(solution)/shard_map/all_to_all | solution.py:100
  158.2 20.2 %all-to-all-start.2 = ((f32[64,1,250]{2,1,0:T(1,128)}), f32[64,1,250]{2,1,0:T(1,128)S(1)}, u32[]{:S(2)}, u32[]{:S(2)}) async-start(f32[64,1,250]{2,1,0:T(1,128)} %broadcast_in_dim.10), calls=%async_computation.2 | async-start | bytes 131072 | tf_op jit(solution)/shard_map/all_to_all | solution.py:20
  188.2 52.3 %all-to-all-start.3 = ((f32[4,1,250,1024]{3,1,2,0:T(1,128)}), f32[4,1,250,1024]{3,1,2,0:T(1,128)}, u32[]{:S(2)}, u32[]{:S(2)}) async-start(f32[4,1,250,1024]{3,1,2,0:T(1,128)} %copy.32), calls=%async_computation.3 | async-start | bytes 8192000 | tf_op jit(solution)/shard_map/all_to_all | solution.py:111
  195.2 8.6 %copy-start.4 = (s32[4,250]{1,0:T(4,128)S(1)}, s32[4,250]{1,0:T(4,128)}, u32[]{:S(2)}) copy-start(s32[4,250]{1,0:T(4,128)} %param.7) | copy-start | bytes 12004
  240.5 7.1 %copy-start.1 = (f32[320,1024]{1,0:T(8,128)S(1)}, f32[320,1024]{1,0:T(8,128)}, u32[]{:S(2)}) copy-start(f32[320,1024]{1,0:T(8,128)} %convolution_add_fusion) | copy-start | bytes 3932164
  240.5 7.1 %copy-start.2 = (f32[320,1024]{1,0:T(8,128)S(1)}, f32[320,1024]{1,0:T(8,128)}, u32[]{:S(2)}) copy-start(f32[320,1024]{1,0:T(8,128)} %convolution_add_fusion.1) | copy-start | bytes 3932164
  240.5 7.2 %copy-start.3 = (f32[320,1024]{1,0:T(8,128)S(1)}, f32[320,1024]{1,0:T(8,128)}, u32[]{:S(2)}) copy-start(f32[320,1024]{1,0:T(8,128)} %convolution_add_fusion.2) | copy-start | bytes 3932164
  251.5 3.3 %copy-start = (f32[3,320,1024]{2,1,0:T(8,128)}, f32[3,320,1024]{2,1,0:T(8,128)S(1)}, u32[]{:S(2)}) copy-start(f32[3,320,1024]{2,1,0:T(8,128)S(1)} %pad_maximum_fusion.1) | copy-start | bytes 11796484
